TPU v7x, 32 devices: a 4x4x1 block of a 4x4x8 slice. The times are simulated.
32 devices in a mesh: rep: 1 (over z), dp: 32 (over x, y, core).
Axes of the slice: x: 4, y: 4, z: 1, core: 2. Of those that a mesh axis runs over, the one named last changes fastest.
The devices are a block of a 4x4x8 slice.
Arguments:
- a: bfloat16 [32, 2, 4096, 896], P(('rep', 'dp'))
- g: bfloat16 [32, 2, 4096, 2304], P(('rep', 'dp'))
Outputs:
- output: bfloat16 [2, 896, 2304], P('rep')
All inputs are finite; a program needn't handle non-finite values.
Results may differ from a plain program's by a relative error of at most 0.012.
Values are sent between devices in bfloat16 or wider.
A program may use at most 768 MiB of HBM per device.

v0:
```python
import jax
import jax.numpy as jnp


def solution(mesh):
    groups = mesh.shape["rep"]

    def step(a, g):
        a, g = (t.reshape(groups, -1, *t.shape[1:]) for t in (a, g))
        sums = jnp.einsum("rsntd,rsntf->rndf", a, g, preferred_element_type=jnp.float32)
        return sums.astype(jnp.bfloat16).reshape(-1, *sums.shape[2:])

    return step
```

profile of v0, /device:TPU:97, one launch (start us, length us, event | category | flops | bytes accessed | tf_op | source)
XLA Modules:
  0.0 175.5 jit_solution(68552392389658649)
XLA Ops:
  0.0 42.6 %fusion = f32[2,896,2304]{2,1,0:T(8,128)} fusion(bf16[1,2,4096,2304]{3,2,1,0:T(8,128)(2,1)} %param.1, bf16[1,2,4096,896]{3,2,1,0:T(8,128)(2,1)} %param), kind=kOutput, calls=%fused_computation | convolution fusion | flops 33822867456 | bytes 68943872 | tf_op jit(solution)/rsntd,rsntf->rndf/dot_general | solution.py:10
  42.6 133.0 %all-reduce.2 = bf16[2,896,2304]{2,1,0:T(8,128)(2,1)} all-reduce(f32[2,896,2304]{2,1,0:T(8,128)} %fusion), channel_id=1, replica_groups=mesh['axis_0'=32] {'axis_0'}, use_global_device_ids=true, to_apply=%add.clone | all-reduce | flops 4128768 | bytes 24772608 | tf_op jit(solution)/rsntd,rsntf->rndf/dot_general | solution.py:10
where the time goes:
time: 176 us
  blocking collectives  133 us (76%)
  matrix products  42.6 us (24%)
    dot_general x1, blocking collectives, step(): jnp.einsum('rsntd,rsntf->rndf', a, g, preferred_element_type=jnp.float32)  133 us
    dot_general x1, matrix products, step(): jnp.einsum('rsntd,rsntf->rndf', a, g, preferred_element_type=jnp.float32)  42.6 us

commit v1 on v0

v1 whole, which is shorter than its diff:
```python
import functools
import math

import jax
import jax.numpy as jnp
from jax import lax
from jax.experimental import pallas as pl
from jax.experimental.pallas import tpu as pltpu
from jax.sharding import PartitionSpec as P

BF, F32 = jnp.bfloat16, jnp.float32
W = 128
HEAD = 3
TB = 512
TB1 = 1024
LAG = dict(A=0, B=1, C=3, D=5, E=7, F=9, G=11, H=13, I=15, J=17, L=19)
RING = 5


def kernel(n, mats, tokens, rows, cols, a_ref, g_ref, o_ref,
           at, ast, gb, gh, acc, xs, xr, cs, sb, rb, ps, tb, ub,
           asem, gsem, ss, rs):
    side = math.isqrt(n // 2)
    per = cols // (2 * W)
    K = mats * per
    me = lax.axis_index("dp")
    c = lax.rem(me, 2)
    y = lax.rem(me // 2, side)
    x = me // (2 * side)
    p = x * (1 - c) + y * c
    q = y * (1 - c) + x * c

    def dev(p_, q_, c_):
        x_ = p_ * (1 - c) + q_ * c
        y_ = q_ * (1 - c) + p_ * c
        return (x_ * side + y_) * 2 + c_

    def at_pos(v, d):
        return lax.rem(v + d + side, side)

    partner = dev(p, q, 1 - c)

    def remote(i, k, src, dst, to):
        return pltpu.make_async_remote_copy(
            src_ref=src, dst_ref=dst, send_sem=ss.at[i, k], recv_sem=rs.at[i, k],
            device_id={"dp": to}, device_id_type=pl.DeviceIdType.MESH)

    def send(i, k, src, dst, to):
        remote(i, k, src, dst, to).start()

    def recv(i, k, dst):
        remote(i, k, dst, dst, partner).wait_recv()

    def sent(i, k, src):
        remote(i, k, src, src, partner).wait_send()

    def dirs(k):
        d = 1 - 2 * lax.rem(k, 2)
        return d

    def stage_a(k):
        xs[k] = acc[lax.rem(k, 4), 1 - c].astype(BF)
        send(0, k, xs.at[k], xr.at[k], partner)

    def stage_b(k):
        d = dirs(k)
        f, b, o = at_pos(p, d), at_pos(p, -d), at_pos(p, 2)
        recv(0, k, xr.at[k])
        s = lax.rem(k, RING)

        def part(i):
            r = pl.ds(pl.multiple_of(i * (rows // side), rows // side), rows // side)
            return acc[lax.rem(k, 4), c, r, :] + xr[k, r, :].astype(F32)

        sb[k, 0] = part(o).astype(BF)
        send(1, k, sb.at[k, 0], rb.at[k, 0], dev(f, q, c))
        sb[k, 1] = part(b).astype(BF)
        send(2, k, sb.at[k, 1], rb.at[k, 1], dev(b, q, c))
        cs[s, 0] = part(f)
        cs[s, 1] = part(p)

    def stage_c(k):
        d = dirs(k)
        s = lax.rem(k, RING)
        recv(1, k, rb.at[k, 0])
        sb[k, 2] = (cs[s, 0] + rb[k, 0].astype(F32)).astype(BF)
        send(3, k, sb.at[k, 2], rb.at[k, 2], dev(at_pos(p, d), q, c))

    def stage_d(k):
        d = dirs(k)
        s = lax.rem(k, RING)
        f, b, o = at_pos(q, d), at_pos(q, -d), at_pos(q, 2)
        recv(2, k, rb.at[k, 1])
        recv(3, k, rb.at[k, 2])
        tot = cs[s, 1] + rb[k, 1].astype(F32) + rb[k, 2].astype(F32)
        ps[s] = tot.reshape(ps.shape[1:])
        tb[k, 0] = ps[s, o].astype(BF)
        send(4, k, tb.at[k, 0], ub.at[k, 0], dev(p, f, c))
        tb[k, 1] = ps[s, b].astype(BF)
        send(5, k, tb.at[k, 1], ub.at[k, 1], dev(p, b, c))

    def stage_e(k):
        f = at_pos(q, dirs(k))
        s = lax.rem(k, RING)
        recv(4, k, ub.at[k, 0])
        tb[k, 2] = (ps[s, f] + ub[k, 0].astype(F32)).astype(BF)
        send(6, k, tb.at[k, 2], ub.at[k, 2], dev(p, f, c))

    def stage_f(k):
        d = dirs(k)
        s = lax.rem(k, RING)
        recv(5, k, ub.at[k, 1])
        recv(6, k, ub.at[k, 2])
        o_ref[k, c, p, q] = (ps[s, q] + ub[k, 1].astype(F32) + ub[k, 2].astype(F32)).astype(BF)
        mine = o_ref.at[k, c, p, q]
        send(7, k, mine, mine, dev(p, at_pos(q, d), c))
        send(8, k, mine, mine, dev(p, at_pos(q, -d), c))

    def stage_g(k):
        d = dirs(k)
        piece = o_ref.at[k, c, p, at_pos(q, -d)]
        recv(7, k, piece)
        send(9, k, piece, piece, dev(p, at_pos(q, d), c))

    def stage_h(k):
        d = dirs(k)
        recv(8, k, o_ref.at[k, c, p, at_pos(q, d)])
        recv(9, k, o_ref.at[k, c, p, at_pos(q, 2)])
        mine = o_ref.at[k, c, p]
        send(10, k, mine, mine, dev(at_pos(p, d), q, c))
        send(11, k, mine, mine, dev(at_pos(p, -d), q, c))
        send(13, k, mine, mine, partner)

    def stage_i(k):
        d = dirs(k)
        piece = o_ref.at[k, c, at_pos(p, -d)]
        recv(10, k, piece)
        send(12, k, piece, piece, dev(at_pos(p, d), q, c))
        send(14, k, piece, piece, partner)
        piece = o_ref.at[k, c, at_pos(p, d)]
        recv(11, k, piece)
        send(15, k, piece, piece, partner)

    def stage_j(k):
        piece = o_ref.at[k, c, at_pos(p, 2)]
        recv(12, k, piece)
        send(16, k, piece, piece, partner)

    def stage_l(k):
        d = dirs(k)
        for i, v in ((13, 0), (14, -d), (15, d), (16, 2)):
            recv(i, k, o_ref.at[k, 1 - c, at_pos(q, v)])
        sent(0, k, xs.at[k])
        for i in range(3):
            sent(1 + i, k, sb.at[k, i])
            sent(4 + i, k, tb.at[k, i])
        sent(7, k, o_ref.at[k, c, p, q])
        sent(8, k, o_ref.at[k, c, p, q])
        sent(9, k, o_ref.at[k, c, p, at_pos(q, -d)])
        sent(10, k, o_ref.at[k, c, p])
        sent(11, k, o_ref.at[k, c, p])
        sent(12, k, o_ref.at[k, c, at_pos(p, -d)])
        sent(13, k, o_ref.at[k, c, p])
        sent(14, k, o_ref.at[k, c, at_pos(p, -d)])
        sent(15, k, o_ref.at[k, c, at_pos(p, d)])
        sent(16, k, o_ref.at[k, c, at_pos(p, 2)])

    stages = [("A", stage_a), ("L", stage_l), ("J", stage_j), ("I", stage_i), ("H", stage_h), ("G", stage_g),
              ("F", stage_f), ("E", stage_e), ("D", stage_d), ("C", stage_c), ("B", stage_b)]

    def service(t, lo, hi):
        for name, fn in stages:
            lag = LAG[name]
            if hi - 1 - lag < 0 or lo - lag >= K:
                continue
            if lo - lag >= 0 and hi - 1 - lag < K:
                fn(t - lag)
            else:
                pl.when((t >= lag) & (t < K + lag))(functools.partial(fn, t - lag))

    def steps(lo, hi, body):
        def run(t, _):
            body(t)
            service(t, lo, hi)
            return 0
        lax.fori_loop(lo, hi, run, 0)

    barrier = pltpu.get_barrier_semaphore()
    for to in (partner, dev(at_pos(p, 1), q, c), dev(at_pos(p, -1), q, c),
               dev(p, at_pos(q, 1), c), dev(p, at_pos(q, -1), c)):
        pl.semaphore_signal(barrier, inc=1, device_id={"dp": to}, device_id_type=pl.DeviceIdType.MESH)

    def gcopy(k):
        s = lax.rem(k, 2)
        return pltpu.make_async_copy(
            g_ref.at[0, k // per, :, pl.ds(pl.multiple_of(lax.rem(k, per) * 2 * W, 2 * W), 2 * W)], gb.at[s], gsem.at[s])

    def ghead(b):
        s = lax.rem(b, 2)
        return pltpu.make_async_copy(
            g_ref.at[0, 0, pl.ds(pl.multiple_of(b * TB, TB), TB), pl.ds(0, HEAD * 2 * W)], gh.at[s], gsem.at[s])

    def acopy(m, b, size):
        s = lax.rem(b, 2)
        return pltpu.make_async_copy(
            a_ref.at[0, m, pl.ds(pl.multiple_of(b * size, size), size), :], ast.at[s, pl.ds(0, size)], asem.at[s])

    nb = tokens // TB
    acopy(0, 0, TB).start()
    ghead(0).start()
    acc[0:HEAD] = jnp.zeros_like(acc[0:HEAD])

    def head(b, _):
        s = lax.rem(b, 2)
        @pl.when(b + 1 < nb)
        def _():
            acopy(0, b + 1, TB).start()
            ghead(b + 1).start()
        acopy(0, b, TB).wait()
        ghead(b).wait()
        t = ast[s, 0:TB].T
        at[0, :, pl.ds(pl.multiple_of(b * TB, TB), TB)] = t
        res = jnp.dot(t, gh[s], preferred_element_type=F32)
        for h in range(HEAD):
            for i in range(2):
                acc[h, i] += res[:, (2 * h + i) * W:(2 * h + i + 1) * W]
        return 0

    lax.fori_loop(0, nb, head, 0)
    acopy(1, 0, TB1).start()
    gcopy(HEAD).start()
    pl.semaphore_wait(barrier, 5)

    def compute(t, m):
        s = lax.rem(t, 2)
        res = jnp.dot(at[m], gb[s], preferred_element_type=F32)
        acc[lax.rem(t, 4), 0] = res[:, :W]
        acc[lax.rem(t, 4), 1] = res[:, W:]

    def with_transpose(t):
        s = lax.rem(t, 2)
        b = t - HEAD
        gcopy(t + 1).start()
        @pl.when(b + 1 < tokens // TB1)
        def _():
            acopy(1, b + 1, TB1).start()
        acopy(1, b, TB1).wait()
        gcopy(t).wait()
        at[1, :, pl.ds(pl.multiple_of(b * TB1, TB1), TB1)] = ast[lax.rem(b, 2)].T
        compute(t, 0)

    def plain(t):
        @pl.when(t + 1 < K)
        def _():
            gcopy(t + 1).start()
        gcopy(t).wait()
        compute(t, t // per)

    for t in range(HEAD):
        service(t, t, t + 1)
    mid = HEAD + tokens // TB1
    steps(HEAD, mid, with_transpose)
    steps(mid, K, plain)
    steps(K, K + LAG["L"], lambda t: None)


def write(o_ref, out_ref, sem):
    blocks, rows, w = o_ref.shape
    per = blocks // out_ref.shape[0]

    def copy(k):
        return pltpu.make_async_copy(
            o_ref.at[k], out_ref.at[k // per, :, pl.ds(k % per * w, w)], sem.at[k])

    for k in range(blocks):
        copy(k).start()
    for k in range(blocks):
        copy(k).wait()


def solution(mesh):
    n = mesh.shape["dp"]
    side = math.isqrt(n // 2)

    def step(a, g):
        _, mats, tokens, rows = a.shape
        cols = g.shape[-1]
        K = mats * cols // (2 * W)
        quarter, piece = rows // side, rows // side // side
        o = pl.pallas_call(
            functools.partial(kernel, n, mats, tokens, rows, cols),
            out_shape=pltpu.VMEM((K, 2, side, side, piece, W), BF),
            in_specs=[pl.BlockSpec(memory_space=pl.ANY)] * 2,
            out_specs=pl.BlockSpec(memory_space=pltpu.VMEM),
            scratch_shapes=[
                pltpu.VMEM((mats, rows, tokens), BF),
                pltpu.VMEM((2, TB1, rows), BF),
                pltpu.VMEM((2, tokens, 2 * W), BF),
                pltpu.VMEM((2, TB, HEAD * 2 * W), BF),
                pltpu.VMEM((4, 2, rows, W), F32),
                pltpu.VMEM((K, rows, W), BF),
                pltpu.VMEM((K, rows, W), BF),
                pltpu.VMEM((RING, 2, quarter, W), F32),
                pltpu.VMEM((K, 3, quarter, W), BF),
                pltpu.VMEM((K, 3, quarter, W), BF),
                pltpu.VMEM((RING, side, piece, W), F32),
                pltpu.VMEM((K, 3, piece, W), BF),
                pltpu.VMEM((K, 3, piece, W), BF),
                pltpu.SemaphoreType.DMA((2,)),
                pltpu.SemaphoreType.DMA((2,)),
                pltpu.SemaphoreType.DMA((17, K)),
                pltpu.SemaphoreType.DMA((17, K)),
            ],
            name="sums",
            compiler_params=pltpu.CompilerParams(
                collective_id=0, has_side_effects=True, vmem_limit_bytes=54 * 2**20),
        )(a, g)
        o = o.reshape(K * 2, rows, W)
        return pl.pallas_call(
            write,
            out_shape=jax.ShapeDtypeStruct((mats, rows, cols), BF),
            in_specs=[pl.BlockSpec(memory_space=pltpu.VMEM)],
            out_specs=pl.BlockSpec(memory_space=pl.ANY),
            scratch_shapes=[pltpu.SemaphoreType.DMA((K * 2,))],
            name="write",
            compiler_params=pltpu.CompilerParams(vmem_limit_bytes=8 * 2**20),
        )(pltpu.with_memory_space_constraint(o, pltpu.VMEM))

    return jax.shard_map(
        step, mesh=mesh, in_specs=(P(("rep", "dp")), P(("rep", "dp"))), out_specs=P("rep"), check_vma=False)
```

time: 176 us -> 100 us (0.57)
  blocking collectives: 133 us -> 0 us
  Pallas kernels: 0 us -> 100 us
  matrix products: 42.6 us -> 0 us
    dot_general x1 -> x0, blocking collectives: 133 us -> none  [step(): jnp.einsum('rsntd,rsntf->rndf', a, g, preferred_element_type=jnp.float32)]
    pallas_call x0 -> x2, Pallas kernels: none -> 100 us  [the longest x1 96.5 us: step(): pl.pallas_call(functools.partial(kernel, n, mats, tokens, rows, cols), ou...]
    dot_general x1 -> x0, matrix products: 42.6 us -> none  [step(): jnp.einsum('rsntd,rsntf->rndf', a, g, preferred_element_type=jnp.float32)]
where the time goes in v1:
time: 100 us
  Pallas kernels  100 us (100%)
    pallas_call x1, Pallas kernels, step(): pl.pallas_call(functools.partial(kernel, n, mats, tokens, rows, cols), ou...  96.5 us
    pallas_call x1, Pallas kernels, step(): pl.pallas_call(write, out_shape=jax.ShapeDtypeStruct((mats, rows, cols),...  3.55 us

profile of v1, /device:TPU:97, one launch (start us, length us, event | category | flops | bytes accessed | tf_op | source)
XLA Modules:
  0.0 100.1 jit_solution(41991939390685960)
XLA Ops:
  0.0 96.5 %sums.1 = bf16[18,2,4,4,56,128]{5,4,3,2,1,0:T(8,128)(2,1)S(1)} custom-call(bf16[1,2,4096,896]{3,2,1,0:T(8,128)(2,1)} %a_ref.1, bf16[1,2,4096,2304]{3,2,1,0:T(8,128)(2,1)} %g_ref.1), custom_call_target="tpu_custom_call" | custom-call | tf_op jit(solution)/shard_map/sums/pallas_call | solution.py:290
  96.5 3.5 %write.1 = bf16[2,896,2304]{2,1,0:T(8,128)(2,1)} custom-call(bf16[36,896,128]{2,1,0:T(8,128)(2,1)S(1)} %bitcast.1), custom_call_target="tpu_custom_call" | custom-call | tf_op jit(solution)/shard_map/write/pallas_call | solution.py:319

commit v2 on v0

v2 whole, which is shorter than its diff:
```python
import functools
import math

import jax
import jax.numpy as jnp
from jax import lax
from jax.experimental import pallas as pl
from jax.experimental.pallas import tpu as pltpu
from jax.sharding import PartitionSpec as P

BF, F32 = jnp.bfloat16, jnp.float32
W = 128
TB = 512
RING = 4
KINDS = "ABCDFHIP"
SLOTS = 6
DIRECT, SPREAD, FUSED = (0, 1, 2, 3, 15, 16, 17,), (16, 17,), ()
STEPS = (
    (),
    (),
    ("b0",),
    ("b1",),
    (),
    ("b2", "B3",),
    ("d0", "b4", "d1",),
    ("b5", "d3",),
    ("d2", "B6",),
    ("c4", "B7", "f0", "f1",),
    ("c6", "f3", "b8", "C5",),
    ("B9", "c7", "f2",),
    ("d4", "B10", "d5", "H0", "H1",),
    ("B11", "C9", "C8", "H3", "d6",),
    ("H2", "B12", "d7", "C10",),
    ("F4", "F5", "I0", "D8", "c11", "B13", "I1",),
    ("C12", "D9", "B14", "F6", "I2", "B15", "I3",),
    ("C13", "D11", "D10", "H5", "D12", "C14", "F8", "F7", "b16", "H4",),
)
DRAIN = (
    "F11", "D15", "D14", "D13", "B17", "F12", "F9", "D16", "H6", "I4", "J1", "J2", "I5", "F15", "H11", "F14", "F10",
    "H7", "H9", "H8", "D17", "F16", "H15", "J0", "J4", "F13", "L2", "H12", "H10", "H14", "I6", "I9", "F17", "I8", "I7",
    "J3", "H13", "I15", "H16", "I14", "I10", "I11", "H17", "J15", "I13", "J8", "I12", "J7", "L1", "J10", "J16", "L15",
    "J11", "J9", "J14", "L9", "L4", "J5", "J17", "L10", "L11", "L16", "L3", "L7", "L14", "L8", "J13", "J6", "J12",
    "L17", "L0", "L5", "L6", "L13", "L12",
)


def kernel(n, mats, tokens, rows, cols, a_ref, g_ref, o_ref,
           at, ast, gb, acc, xs, xr, cs, sb, rb, ps, tb, ub, fr,
           asem, gsem, ss, rs):
    side = math.isqrt(n // 2)
    per = cols // (2 * W)
    K = mats * per
    me = lax.axis_index("dp")
    c = lax.rem(me, 2)
    y = lax.rem(me // 2, side)
    x = me // (2 * side)
    p = x * (1 - c) + y * c
    q = y * (1 - c) + x * c

    def dev(p_, q_, c_):
        x_ = p_ * (1 - c) + q_ * c
        y_ = q_ * (1 - c) + p_ * c
        return (x_ * side + y_) * 2 + c_

    ppos = [lax.rem(p + j, side) for j in range(side)]
    qpos = [lax.rem(q + j, side) for j in range(side)]
    pdev = [dev(v, q, c) for v in ppos]
    qdev = [dev(p, v, c) for v in qpos]
    partner = dev(p, q, 1 - c)

    def pick(vals, k, way):
        u, v = (vals[1], vals[side - 1]) if way > 0 else (vals[side - 1], vals[1])
        return v if k % 2 else u

    def remote(kind, slot, i, k, src, dst, to):
        return pltpu.make_async_remote_copy(
            src_ref=src, dst_ref=dst, send_sem=ss.at[KINDS.index(kind), slot], recv_sem=rs.at[i, k],
            device_id={"dp": to}, device_id_type=pl.DeviceIdType.MESH)

    flying = {kind: [] for kind in KINDS}
    count = {kind: 0 for kind in KINDS}

    def land(kind):
        slot = (count[kind] - len(flying[kind])) % SLOTS
        size = flying[kind].pop(0)
        remote(kind, slot, 0, 0, size, size, partner).wait_send()

    def send(kind, k, size, *copies):
        if len(flying[kind]) == SLOTS:
            land(kind)
        for i, src, dst, to in copies:
            remote(kind, count[kind] % SLOTS, i, k, src, dst, to).start()
        flying[kind].append(size)
        count[kind] += 1

    def recv(i, k, size):
        remote("A", 0, i, k, size, size, partner).wait_recv()

    def quarter(i):
        return pl.ds(pl.multiple_of(i * (rows // side), rows // side), rows // side)

    quarters = [None] + [rb.at[0, pl.ds(0, m)] for m in (1, 2, 3)]
    half, pieces = xr.at[0], ub.at[0]

    def send_a(k):
        send("A", k, half, (0, xs.at[k], xr.at[k], partner))

    def wait_b(k):
        recv(0, k, half)

    def work_b(k):
        def part(i):
            return acc[k % RING, quarter(i), :] + xr[k, quarter(i), :].astype(F32)

        if k in DIRECT:
            for j in (2, 1, 3):
                sb[k, j - 1] = part(ppos[j]).astype(BF)
        else:
            sb[k, 0] = part(ppos[2]).astype(BF)
            sb[k, 1] = part(pick(ppos, k, -1)).astype(BF)
            cs[k, 0] = part(pick(ppos, k, 1))
        cs[k, 1] = part(p)

    def send_b(k):
        if k in DIRECT:
            send("B", k, quarters[3], *((2, sb.at[k, j - 1], rb.at[k, j - 1], pdev[j]) for j in (2, 1, 3)))
        else:
            send("B", k, quarters[2], (1, sb.at[k, 0], rb.at[k, 0], pick(pdev, k, 1)),
                 (2, sb.at[k, 1], rb.at[k, 1], pick(pdev, k, -1)))

    def wait_c(k):
        recv(1, k, quarters[1])

    def work_c(k):
        sb[k, 2] = (cs[k, 0] + rb[k, 0].astype(F32)).astype(BF)

    def send_c(k):
        send("C", k, quarters[1], (2, sb.at[k, 2], rb.at[k, 2], pick(pdev, k, 1)))

    def wait_d(k):
        recv(2, k, quarters[3 if k in DIRECT else 2])

    def work_d(k):
        tot = cs[k, 1] + rb[k, 1].astype(F32) + rb[k, 2].astype(F32)
        if k in DIRECT:
            tot = tot + rb[k, 0].astype(F32)
        if k in FUSED:
            fr[FUSED.index(k), q] = tot.astype(BF)
            return
        ps[k] = tot.reshape(ps.shape[1:])
        for j in (2, 1, 3):
            tb[k, j - 1] = ps[k, qpos[j]].astype(BF)

    def send_d(k):
        if k in FUSED:
            mine = fr.at[FUSED.index(k), q]
            send("D", k, quarters[3], *((4, mine, mine, qdev[j]) for j in (2, 1, 3)))
        else:
            send("D", k, pieces, *((3, tb.at[k, j - 1], ub.at[k, j - 1], qdev[j]) for j in (2, 1, 3)))

    def wait_f(k):
        recv(3, k, pieces)

    def work_f(k):
        tot = ps[k, q] + ub[k, 0].astype(F32) + ub[k, 1].astype(F32) + ub[k, 2].astype(F32)
        o_ref[k, c, p, q] = tot.astype(BF)

    def send_f(k):
        mine = o_ref.at[k, c, p, q]
        send("F", k, pieces, *((4, mine, mine, qdev[j]) for j in (2, 1, 3)))

    def wait_h(k):
        recv(4, k, quarters[3] if k in FUSED else pieces)

    def work_h(k):
        if k in FUSED:
            f = FUSED.index(k)
            tot = fr[f, 0].astype(F32)
            for j in range(1, side):
                tot = tot + fr[f, j].astype(F32)
            o_ref[k, c, p] = tot.reshape(o_ref.shape[3:]).astype(BF)

    def across(k, j, to, i=7):
        quad = o_ref.at[k, c, ppos[j] if isinstance(j, int) else j]
        return i, quad, quad, to

    def send_h(k):
        if k in SPREAD:
            send("H", k, quarters[3], *(across(k, 0, pdev[j], 6) for j in (2, 1, 3)))
        else:
            send("H", k, quarters[2], *(across(k, 0, pdev[j], 5) for j in (1, side - 1)))
        send("P", k, quarters[1], across(k, 0, partner))

    def stage_i(k):
        recv(5, k, quarters[2])
        send("I", k, quarters[1], across(k, pick(ppos, k, -1), pick(pdev, k, 1), 6))
        send("P", k, quarters[2], across(k, 1, partner), across(k, side - 1, partner))

    def stage_j(k):
        if k in SPREAD:
            recv(6, k, quarters[3])
            send("P", k, quarters[3], *(across(k, j, partner) for j in (1, 2, 3)))
        else:
            recv(6, k, quarters[1])
            send("P", k, quarters[1], across(k, 2, partner))

    def stage_l(k):
        recv(7, k, half)

    waits = dict(B=wait_b, C=wait_c, D=wait_d, F=wait_f, H=wait_h)
    works = dict(B=work_b, C=work_c, D=work_d, F=work_f, H=work_h)
    sends = dict(A=send_a, B=send_b, C=send_c, D=send_d, F=send_f, H=send_h)
    whole = dict(I=stage_i, J=stage_j, L=stage_l)

    def stage(name, k):
        if name in whole:
            whole[name](k)
        else:
            waits[name](k)
            works[name](k)
            sends[name](k)

    barrier = pltpu.get_barrier_semaphore()
    for to in [partner] + pdev[1:] + qdev[1:]:
        pl.semaphore_signal(barrier, inc=1, device_id={"dp": to}, device_id_type=pl.DeviceIdType.MESH)

    def gcopies(k):
        def half(i):
            col = pl.multiple_of((2 * (k % per) + lax.rem(c + i, 2)) * W, W)
            return pltpu.make_async_copy(
                g_ref.at[0, k // per, :, pl.ds(col, W)], gb.at[k % 2, :, pl.ds(i * W, W)], gsem.at[i, k % 2])
        return half(0), half(1)

    def acopy(m, b):
        return pltpu.make_async_copy(a_ref.at[0, m, pl.ds(b * TB, TB), :], ast.at[b], asem.at[b])

    def turn(m, b):
        at[m, :, pl.ds(b * TB if isinstance(b, int) else pl.multiple_of(b * TB, TB), TB)] = ast[b].T

    nb = tokens // TB
    for b in range(nb):
        acopy(0, b).start()
    for copy in gcopies(0):
        copy.start()
    with jax.named_scope("head"):
        def first(b, _):
            acopy(0, b).wait()
            turn(0, b)
            acopy(1, b).start()
            return 0
        lax.fori_loop(0, nb, first, 0)
    pl.semaphore_wait(barrier, 1 + 2 * (side - 1))

    done = 0
    for t in range(K):
        with jax.named_scope("top"):
            for copy in gcopies(t + 1) if t + 1 < K else ():
                copy.start()
            beside = []
            for item in STEPS[t]:
                name, k = item[0].upper(), int(item[1:])
                if item[0] == name:
                    stage(name, k)
                else:
                    waits[name](k)
                    beside.append((name, k))
            turns = range(done, min(done + 2, nb))
            done += len(turns)
            for b in turns:
                acopy(1, b).wait()
            for copy in gcopies(t):
                copy.wait()
        with jax.named_scope("dot"):
            @pl.when(me >= 0)
            def _():
                for b in turns:
                    turn(1, b)
                for name, k in beside:
                    works[name](k)
                res = jnp.dot(at[t // per], gb[t % 2], preferred_element_type=F32)
                acc[t % RING] = res[:, :W]
                xs[t] = res[:, W:].astype(BF)
        with jax.named_scope("end"):
            send_a(t)
            for name, k in beside:
                sends[name](k)
    for item in DRAIN:
        with jax.named_scope(item):
            stage(item[0], int(item[1:]))
    for kind in KINDS:
        while flying[kind]:
            land(kind)


def write(o_ref, out_ref, sem):
    w = o_ref.shape[-1]
    per = out_ref.shape[2] // w
    blocks = out_ref.shape[0] * per

    def copy(k):
        return pltpu.make_async_copy(
            o_ref.at[k], out_ref.at[k // per, :, pl.ds(k % per * w, w)], sem.at[k])

    for k in range(blocks):
        copy(k).start()
    for k in range(blocks):
        copy(k).wait()


def solution(mesh):
    n = mesh.shape["dp"]
    side = math.isqrt(n // 2)

    def step(a, g):
        _, mats, tokens, rows = a.shape
        cols = g.shape[-1]
        K = mats * cols // (2 * W)
        quarter, piece = rows // side, rows // side // side
        o = pl.pallas_call(
            functools.partial(kernel, n, mats, tokens, rows, cols),
            out_shape=pltpu.VMEM((K, 2, side, side, piece, W), BF),
            in_specs=[pl.BlockSpec(memory_space=pl.ANY)] * 2,
            out_specs=pl.BlockSpec(memory_space=pltpu.VMEM),
            scratch_shapes=[
                pltpu.VMEM((mats, rows, tokens), BF),
                pltpu.VMEM((tokens // TB, TB, rows), BF),
                pltpu.VMEM((2, tokens, 2 * W), BF),
                pltpu.VMEM((RING, rows, W), F32),
                pltpu.VMEM((K, rows, W), BF),
                pltpu.VMEM((K, rows, W), BF),
                pltpu.VMEM((K, 2, quarter, W), F32),
                pltpu.VMEM((K, 3, quarter, W), BF),
                pltpu.VMEM((K, 3, quarter, W), BF),
                pltpu.VMEM((K, side, piece, W), F32),
                pltpu.VMEM((K, 3, piece, W), BF),
                pltpu.VMEM((K, 3, piece, W), BF),
                pltpu.VMEM((max(len(FUSED), 1), side, quarter, W), BF),
                pltpu.SemaphoreType.DMA((tokens // TB,)),
                pltpu.SemaphoreType.DMA((2, 2)),
                pltpu.SemaphoreType.DMA((len(KINDS), SLOTS)),
                pltpu.SemaphoreType.DMA((8, K)),
            ],
            name="sums",
            compiler_params=pltpu.CompilerParams(
                collective_id=0, has_side_effects=True, vmem_limit_bytes=55 * 2**20),
        )(a, g)
        o = o.reshape(K * 2, rows, W)
        return pl.pallas_call(
            write,
            out_shape=jax.ShapeDtypeStruct((mats, rows, cols), BF),
            in_specs=[pl.BlockSpec(memory_space=pltpu.VMEM)],
            out_specs=pl.BlockSpec(memory_space=pl.ANY),
            scratch_shapes=[pltpu.SemaphoreType.DMA((K * 2,))],
            name="write",
            compiler_params=pltpu.CompilerParams(vmem_limit_bytes=8 * 2**20),
        )(pltpu.with_memory_space_constraint(o, pltpu.VMEM))

    return jax.shard_map(
        step, mesh=mesh, in_specs=(P(("rep", "dp")), P(("rep", "dp"))), out_specs=P("rep"), check_vma=False)
```

time: 176 us -> 84.6 us (0.48)
  blocking collectives: 133 us -> 0 us
  Pallas kernels: 0 us -> 84.4 us
  matrix products: 42.6 us -> 0 us
    dot_general x1 -> x0, blocking collectives: 133 us -> none  [step(): jnp.einsum('rsntd,rsntf->rndf', a, g, preferred_element_type=jnp.float32)]
    pallas_call x0 -> x2, Pallas kernels: none -> 84.4 us  [the longest x1 80.8 us: step(): pl.pallas_call(functools.partial(kernel, n, mats, tokens, rows, cols), ou...]
    dot_general x1 -> x0, matrix products: 42.6 us -> none  [step(): jnp.einsum('rsntd,rsntf->rndf', a, g, preferred_element_type=jnp.float32)]
where the time goes in v2:
time: 84.6 us
  Pallas kernels  84.4 us (100%)
    pallas_call x1, Pallas kernels, step(): pl.pallas_call(functools.partial(kernel, n, mats, tokens, rows, cols), ou...  80.8 us
    pallas_call x1, Pallas kernels, step(): pl.pallas_call(write, out_shape=jax.ShapeDtypeStruct((mats, rows, cols),...  3.55 us

profile of v2, /device:TPU:97, one launch (start us, length us, event | category | flops | bytes accessed | tf_op | source)
XLA Modules:
  0.0 84.6 jit_solution(11274135980873568710)
XLA Ops:
  0.0 80.8 %sums.1 = bf16[18,2,4,4,56,128]{5,4,3,2,1,0:T(8,128)(2,1)S(1)} custom-call(bf16[1,2,4096,896]{3,2,1,0:T(8,128)(2,1)} %a_ref.1, bf16[1,2,4096,2304]{3,2,1,0:T(8,128)(2,1)} %g_ref.1), custom_call_target="tpu_custom_call" | custom-call | tf_op jit(solution)/shard_map/sums/pallas_call | solution.py:319
  80.8 3.5 %write.1 = bf16[2,896,2304]{2,1,0:T(8,128)(2,1)} custom-call(bf16[36,896,128]{2,1,0:T(8,128)(2,1)S(1)} %bitcast.1), custom_call_target="tpu_custom_call" | custom-call | tf_op jit(solution)/shard_map/write/pallas_call | solution.py:348

commit v3 on v2

v3 whole, which is shorter than its diff:
```python
import functools
import math

import jax
import jax.numpy as jnp
from jax import lax
from jax.experimental import pallas as pl
from jax.experimental.pallas import tpu as pltpu
from jax.sharding import PartitionSpec as P

BF, F32 = jnp.bfloat16, jnp.float32
W = 128
TB = 512
RING = 4
KINDS = "ABDFHP"
DIRECT, SPREAD, NEAR = (0, 1, 2, 3, 4, 5, 6, 7, 8, 15, 16, 17,), (16, 17,), ()
STEPS = (
    (),
    (),
    ("B0",),
    ("b1",),
    ("d0", "b2",),
    ("B3",),
    ("d1", "B4",),
    ("D2", "B5", "f0",),
    ("D3", "B6", "D4",),
    ("F1", "B7", "F2", "D5",),
    ("H0", "d6", "F3", "B8",),
    ("D7", "F4", "B9", "H1", "H2",),
    ("B10", "F5", "H3", "D8",),
    ("H4", "F7", "I0", "C9", "B11", "F6",),
    ("I1", "I2", "H5", "C10", "B12", "I3",),
    ("B13", "D9", "I4", "H7", "C11",),
    ("B14", "f8", "H6", "C12", "C13", "D10", "B15",),
    ("D11", "I5", "C14", "d13", "F9", "J3", "B16", "D12", "I6", "I7",),
)
DRAIN = (
    "F10", "D15", "D14", "B17", "D16", "J0", "F11", "H8", "H9", "F14", "F13", "F15", "D17", "J1", "F12", "H10", "H11",
    "F16", "I9", "J2", "I8", "H13", "F17", "H15", "H14", "I11", "H12", "H16", "I10", "H17", "J4", "I13", "I14", "I15",
    "J8", "I12", "J5", "J6", "J16", "J10", "J11", "J7", "J9", "J14", "J13", "J17", "J12", "J15",
)


def kernel(n, mats, tokens, rows, cols, a_ref, g_ref, o_ref,
           at, ast, t0, t1, gb, acc, first, xs, xr, cs, sb, rb, ps, tb, ub,
           asem, gsem, hsem, ss, rs, rl):
    side = math.isqrt(n // 2)
    per = cols // (2 * W)
    K = mats * per
    me = lax.axis_index("dp")
    c = lax.rem(me, 2)
    y = lax.rem(me // 2, side)
    x = me // (2 * side)
    p = x * (1 - c) + y * c
    q = y * (1 - c) + x * c

    def dev(p_, q_, c_):
        x_ = p_ * (1 - c) + q_ * c
        y_ = q_ * (1 - c) + p_ * c
        return (x_ * side + y_) * 2 + c_

    ppos = [lax.rem(p + j, side) for j in range(side)]
    qpos = [lax.rem(q + j, side) for j in range(side)]
    pdev = [dev(v, q, c) for v in ppos]
    qdev = [dev(p, v, c) for v in qpos]
    partner = dev(p, q, 1 - c)

    def pick(vals, k, way):
        u, v = (vals[1], vals[side - 1]) if way > 0 else (vals[side - 1], vals[1])
        return v if k % 2 else u

    def remote(kind, i, k, src, dst, to):
        return pltpu.make_async_remote_copy(
            src_ref=src, dst_ref=dst, send_sem=ss.at[KINDS.index(kind)], recv_sem=rl if i == 7 else rs.at[i, k],
            device_id={"dp": to}, device_id_type=pl.DeviceIdType.MESH)

    def send(kind, k, *copies):
        for i, src, dst, to in copies:
            remote(kind, i, k, src, dst, to).start()

    def recv(i, k, size):
        remote("A", i, k, size, size, partner).wait_recv()

    lanes = pl.ds(pl.multiple_of(c * W, W), W)

    def quarter(i):
        return pl.ds(pl.multiple_of(i * (rows // side), rows // side), rows // side)

    quarters = [None] + [rb.at[0, pl.ds(0, m)] for m in (1, 2, 3)]
    pieces = [None] + [ub.at[0, pl.ds(0, m)] for m in (1, 2, 3)]
    half = xr.at[0]

    def send_a(k):
        send("A", k, (0, xs.at[k], xr.at[k], partner))

    def wait_b(k):
        recv(0, k, half)

    def work_b(k):
        def part(i):
            return acc[k % RING, quarter(i), :] + xr[k, quarter(i), :].astype(F32)

        if k in DIRECT:
            for j in (2, 1, 3):
                sb[k, j - 1] = part(ppos[j]).astype(BF)
        else:
            sb[k, 0] = part(ppos[2]).astype(BF)
            sb[k, 1] = part(pick(ppos, k, -1)).astype(BF)
            cs[k, 0] = part(pick(ppos, k, 1))
        cs[k, 1] = part(p)

    def send_b(k):
        if k in DIRECT:
            send("B", k, *((2, sb.at[k, j - 1], rb.at[k, j - 1], pdev[j]) for j in (2, 1, 3)))
        else:
            send("B", k, (1, sb.at[k, 0], rb.at[k, 0], pick(pdev, k, 1)),
                 (2, sb.at[k, 1], rb.at[k, 1], pick(pdev, k, -1)))

    def wait_c(k):
        recv(1, k, quarters[1])

    def work_c(k):
        sb[k, 2] = (cs[k, 0] + rb[k, 0].astype(F32)).astype(BF)

    def send_c(k):
        send("B", k, (2, sb.at[k, 2], rb.at[k, 2], pick(pdev, k, 1)))

    def wait_d(k):
        recv(2, k, quarters[3 if k in DIRECT else 2])

    def work_d(k):
        tot = cs[k, 1] + rb[k, 1].astype(F32) + rb[k, 2].astype(F32)
        if k in DIRECT:
            tot = tot + rb[k, 0].astype(F32)
        ps[k] = tot.reshape(ps.shape[1:])
        if k in NEAR:
            tb[k, 1] = ps[k, qpos[2]].astype(BF)
            tb[k, 0] = ps[k, pick(qpos, k, -1)].astype(BF)
        else:
            for j in (2, 1, 3):
                tb[k, j - 1] = ps[k, qpos[j]].astype(BF)

    def send_d(k):
        if k in NEAR:
            send("D", k, (8, tb.at[k, 1], ub.at[k, 1], pick(qdev, k, 1)),
                 (3, tb.at[k, 0], ub.at[k, 0], pick(qdev, k, -1)))
        else:
            send("D", k, *((3, tb.at[k, j - 1], ub.at[k, j - 1], qdev[j]) for j in (2, 1, 3)))

    def wait_e(k):
        recv(8, k, pieces[1])

    def work_e(k):
        tb[k, 2] = (ps[k, pick(qpos, k, 1)] + ub[k, 1].astype(F32)).astype(BF)

    def send_e(k):
        send("D", k, (3, tb.at[k, 2], ub.at[k, 2], pick(qdev, k, 1)))

    def wait_f(k):
        recv(3, k, pieces[2 if k in NEAR else 3])

    def work_f(k):
        tot = ps[k, q] + ub[k, 0].astype(F32) + ub[k, 2].astype(F32)
        if k not in NEAR:
            tot = tot + ub[k, 1].astype(F32)
        o_ref[k, p, q, :, lanes] = tot.astype(BF)

    def send_f(k):
        mine = o_ref.at[k, p, q, :, lanes]
        if k in NEAR:
            send("F", k, (9, mine, mine, pick(qdev, k, 1)), (4, mine, mine, pick(qdev, k, -1)))
        else:
            send("F", k, *((4, mine, mine, qdev[j]) for j in (2, 1, 3)))

    def stage_g(k):
        recv(9, k, pieces[1])
        piece = o_ref.at[k, p, pick(qpos, k, -1), :, lanes]
        send("F", k, (4, piece, piece, pick(qdev, k, 1)))

    def wait_h(k):
        recv(4, k, pieces[2 if k in NEAR else 3])

    def work_h(k):
        pass

    def across(k, j, to, i=7):
        quad = o_ref.at[k, ppos[j] if isinstance(j, int) else j, :, :, lanes]
        return i, quad, quad, to

    def send_h(k):
        if k in SPREAD:
            send("H", k, *(across(k, 0, pdev[j], 6) for j in (2, 1, 3)))
        else:
            send("H", k, *(across(k, 0, pdev[j], 5) for j in (1, side - 1)))
        send("P", k, across(k, 0, partner))

    def stage_i(k):
        recv(5, k, quarters[2])
        send("H", k, across(k, pick(ppos, k, -1), pick(pdev, k, 1), 6))
        send("P", k, across(k, 1, partner), across(k, side - 1, partner))

    def stage_j(k):
        if k in SPREAD:
            recv(6, k, quarters[3])
            send("P", k, *(across(k, j, partner) for j in (1, 2, 3)))
        else:
            recv(6, k, quarters[1])
            send("P", k, across(k, 2, partner))

    waits = dict(B=wait_b, C=wait_c, D=wait_d, E=wait_e, F=wait_f, H=wait_h)
    works = dict(B=work_b, C=work_c, D=work_d, E=work_e, F=work_f, H=work_h)
    sends = dict(A=send_a, B=send_b, C=send_c, D=send_d, E=send_e, F=send_f, H=send_h)
    whole = dict(G=stage_g, I=stage_i, J=stage_j)

    def stage(name, k):
        if name in whole:
            whole[name](k)
        else:
            waits[name](k)
            works[name](k)
            sends[name](k)

    barrier = pltpu.get_barrier_semaphore()
    for to in [partner] + pdev[1:] + qdev[1:]:
        pl.semaphore_signal(barrier, inc=1, device_id={"dp": to}, device_id_type=pl.DeviceIdType.MESH)

    def gcopies(k):
        def half(i):
            col = pl.multiple_of((2 * (k % per) + lax.rem(c + i, 2)) * W, W)
            return pltpu.make_async_copy(
                g_ref.at[0, k // per, :, pl.ds(col, W)], gb.at[k % 2, :, pl.ds(i * W, W)], gsem.at[i, k % 2])
        return half(0), half(1)

    def acopy(m, b):
        return pltpu.make_async_copy(a_ref.at[0, m, pl.ds(b * TB, TB), :], ast.at[b], asem.at[b])

    nb = tokens // TB
    blocks = (t0, t1)

    def hcopies(b):
        return [pltpu.make_async_copy(
            g_ref.at[0, 0, pl.ds(b * TB, TB), pl.ds(pl.multiple_of(lax.rem(c + i, 2) * W, W), W)],
            gb.at[0, pl.ds(b * TB, TB), pl.ds(i * W, W)], hsem.at[i, b]) for i in range(2)]

    for b in range(nb):
        for copy in [acopy(0, b)] + hcopies(b):
            copy.start()
    first[...] = jnp.zeros_like(first)
    with jax.named_scope("head"):
        acopy(0, 0).wait()
        t0[...] = ast[0].T
        at[0, :, 0:TB] = t0[...]

        def head(i, _):
            for s in range(2):
                b = 2 * i + s
                nxt = lax.min(b + 1, nb - 1)

                @pl.when(b + 1 < nb)
                def _():
                    acopy(0, nxt).wait()

                for copy in hcopies(b):
                    copy.wait()

                @pl.when(me >= 0)
                def _():
                    t = ast[nxt].T
                    blocks[1 - s][...] = t
                    at[0, :, pl.ds(pl.multiple_of(nxt * TB, TB), TB)] = t
                    first[...] += jnp.dot(
                        blocks[s][...], gb[0, pl.ds(pl.multiple_of(b * TB, TB), TB)], preferred_element_type=F32)

            @pl.when(i == 1)
            def _():
                for copy in gcopies(1):
                    copy.start()
            return 0

        lax.fori_loop(0, nb // 2, head, 0)
    for copy in gcopies(2):
        copy.start()
    xs[0] = first[:, W:].astype(BF)
    pl.semaphore_wait(barrier, 1 + 2 * (side - 1))
    send_a(0)
    acc[0] = first[:, :W]

    done = 0
    for t in range(1, K):
        with jax.named_scope("top"):
            for copy in gcopies(t + 1) if 1 < t < K - 1 else ():
                copy.start()
            for b in range(2 * t - 2, min(2 * t, nb)):
                acopy(1, b).start()
            beside = []
            for item in STEPS[t]:
                name, k = item[0].upper(), int(item[1:])
                if item[0] == name:
                    stage(name, k)
                else:
                    waits[name](k)
                    beside.append((name, k))
            turns = range(done, min(done + 2, nb)) if t > 2 else ()
            done += len(turns)
            for b in turns:
                acopy(1, b).wait()
            for copy in gcopies(t):
                copy.wait()
        with jax.named_scope("dot"):
            @pl.when(me >= 0)
            def _():
                for b in turns:
                    at[1, :, b * TB:(b + 1) * TB] = ast[b].T
                for name, k in beside:
                    works[name](k)
                res = jnp.dot(at[t // per], gb[t % 2], preferred_element_type=F32)
                acc[t % RING] = res[:, :W]
                xs[t] = res[:, W:].astype(BF)
        with jax.named_scope("end"):
            send_a(t)
            for name, k in beside:
                sends[name](k)
    for item in DRAIN:
        with jax.named_scope(item):
            stage(item[0], int(item[1:]))
    recv(7, 0, xr)
    for kind, size in zip(KINDS, (xs, sb, tb, tb, sb, xs)):
        remote(kind, 0, 0, size, size, partner).wait_send()


def write(o_ref, out_ref, sem):
    w = o_ref.shape[-1]
    per = out_ref.shape[2] // w
    blocks = out_ref.shape[0] * per

    def copy(k):
        return pltpu.make_async_copy(
            o_ref.at[k], out_ref.at[k // per, :, pl.ds(k % per * w, w)], sem.at[k])

    for k in range(blocks):
        copy(k).start()
    for k in range(blocks):
        copy(k).wait()


def solution(mesh):
    n = mesh.shape["dp"]
    side = math.isqrt(n // 2)

    def step(a, g):
        _, mats, tokens, rows = a.shape
        cols = g.shape[-1]
        K = mats * cols // (2 * W)
        quarter, piece = rows // side, rows // side // side
        o = pl.pallas_call(
            functools.partial(kernel, n, mats, tokens, rows, cols),
            out_shape=pltpu.VMEM((K, side, side, piece, 2 * W), BF),
            in_specs=[pl.BlockSpec(memory_space=pl.ANY)] * 2,
            out_specs=pl.BlockSpec(memory_space=pltpu.VMEM),
            scratch_shapes=[
                pltpu.VMEM((mats, rows, tokens), BF),
                pltpu.VMEM((tokens // TB, TB, rows), BF),
                pltpu.VMEM((rows, TB), BF),
                pltpu.VMEM((rows, TB), BF),
                pltpu.VMEM((2, tokens, 2 * W), BF),
                pltpu.VMEM((RING, rows, W), F32),
                pltpu.VMEM((rows, 2 * W), F32),
                pltpu.VMEM((K, rows, W), BF),
                pltpu.VMEM((K, rows, W), BF),
                pltpu.VMEM((K, 2, quarter, W), F32),
                pltpu.VMEM((K, 3, quarter, W), BF),
                pltpu.VMEM((K, 3, quarter, W), BF),
                pltpu.VMEM((K, side, piece, W), F32),
                pltpu.VMEM((K, 3, piece, W), BF),
                pltpu.VMEM((K, 3, piece, W), BF),
                pltpu.SemaphoreType.DMA((tokens // TB,)),
                pltpu.SemaphoreType.DMA((2, 2)),
                pltpu.SemaphoreType.DMA((2, tokens // TB)),
                pltpu.SemaphoreType.DMA((len(KINDS),)),
                pltpu.SemaphoreType.DMA((10 if NEAR else 7, K)),
                pltpu.SemaphoreType.DMA,
            ],
            name="sums",
            compiler_params=pltpu.CompilerParams(
                collective_id=0, has_side_effects=True, vmem_limit_bytes=55 * 2**20),
        )(a, g)
        o = o.reshape(K, rows, 2 * W)
        return pl.pallas_call(
            write,
            out_shape=jax.ShapeDtypeStruct((mats, rows, cols), BF),
            in_specs=[pl.BlockSpec(memory_space=pltpu.VMEM)],
            out_specs=pl.BlockSpec(memory_space=pl.ANY),
            scratch_shapes=[pltpu.SemaphoreType.DMA((K,))],
            name="write",
            compiler_params=pltpu.CompilerParams(vmem_limit_bytes=8 * 2**20),
        )(pltpu.with_memory_space_constraint(o, pltpu.VMEM))

    return jax.shard_map(
        step, mesh=mesh, in_specs=(P(("rep", "dp")), P(("rep", "dp"))), out_specs=P("rep"), check_vma=False)
```

time: 84.6 us -> 81.2 us (0.960)
  Pallas kernels: 84.4 us -> 80.9 us
    pallas_call x1, Pallas kernels: 80.8 us -> 77.5 us  [step(): pl.pallas_call(functools.partial(kernel, n, mats, tokens, rows, cols), ou...]
where the time goes in v3:
time: 81.2 us; the launch traced here: 81.1 us
  Pallas kernels  80.9 us (100%)
    pallas_call x1, Pallas kernels, step(): pl.pallas_call(functools.partial(kernel, n, mats, tokens, rows, cols), ou...  77.5 us
    pallas_call x1, Pallas kernels, step(): pl.pallas_call(write, out_shape=jax.ShapeDtypeStruct((mats, rows, cols),...  3.4 us

profile of v3, /device:TPU:97, one launch (start us, length us, event | category | flops | bytes accessed | tf_op | source)
XLA Modules:
  0.0 81.1 jit_solution(4967241752702094155)
XLA Ops:
  0.0 77.5 %sums.1 = bf16[18,4,4,56,256]{4,3,2,1,0:T(8,128)(2,1)S(1)} custom-call(bf16[1,2,4096,896]{3,2,1,0:T(8,128)(2,1)} %a_ref.1, bf16[1,2,4096,2304]{3,2,1,0:T(8,128)(2,1)} %g_ref.1), custom_call_target="tpu_custom_call" | custom-call | tf_op jit(solution)/shard_map/sums/pallas_call | solution.py:355
  77.5 3.4 %write.1 = bf16[2,896,2304]{2,1,0:T(8,128)(2,1)} custom-call(bf16[18,896,256]{2,1,0:T(8,128)(2,1)S(1)} %bitcast.1), custom_call_target="tpu_custom_call" | custom-call | tf_op jit(solution)/shard_map/write/pallas_call | solution.py:388

commit v4 on v3

--- a/solution.py
+++ b/solution.py
@@ -17,27 +17,27 @@
 STEPS = (
     (),
     (),
-    ("B0",),
+    ("b0",),
     ("b1",),
-    ("d0", "b2",),
-    ("B3",),
-    ("d1", "B4",),
-    ("D2", "B5", "f0",),
-    ("D3", "B6", "D4",),
-    ("F1", "B7", "F2", "D5",),
-    ("H0", "d6", "F3", "B8",),
-    ("D7", "F4", "B9", "H1", "H2",),
-    ("B10", "F5", "H3", "D8",),
-    ("H4", "F7", "I0", "C9", "B11", "F6",),
-    ("I1", "I2", "H5", "C10", "B12", "I3",),
-    ("B13", "D9", "I4", "H7", "C11",),
-    ("B14", "f8", "H6", "C12", "C13", "D10", "B15",),
-    ("D11", "I5", "C14", "d13", "F9", "J3", "B16", "D12", "I6", "I7",),
+    ("b2",),
+    ("d0", "B3",),
+    ("D1", "B4",),
+    ("D2", "B5", "D3",),
+    ("F1", "F0", "B6", "D4",),
+    ("F2", "D5", "B7", "F3", "H1",),
+    ("B8", "f4", "d6", "H0",),
+    ("H2", "D7", "b9", "f5", "H3",),
+    ("B10", "D8", "I0", "I1",),
+    ("B11", "I2", "F7", "F6", "H4", "I3",),
+    ("C10", "C9", "F8", "B12", "H5",),
+    ("B13", "C11", "H7", "I4", "H6", "J2",),
+    ("D9", "B14", "C12", "H8", "D10", "C13",),
+    ("D11", "B15", "I5", "J0", "J3", "F9", "I7", "C14", "D13", "d12", "F10", "B16", "I6",),
 )
 DRAIN = (
-    "F10", "D15", "D14", "B17", "D16", "J0", "F11", "H8", "H9", "F14", "F13", "F15", "D17", "J1", "F12", "H10", "H11",
-    "F16", "I9", "J2", "I8", "H13", "F17", "H15", "H14", "I11", "H12", "H16", "I10", "H17", "J4", "I13", "I14", "I15",
-    "J8", "I12", "J5", "J6", "J16", "J10", "J11", "J7", "J9", "J14", "J13", "J17", "J12", "J15",
+    "D15", "D14", "F11", "J1", "J4", "B17", "F13", "H9", "D16", "H10", "F15", "J5", "F14", "F12", "H11", "D17", "F16",
+    "H13", "H15", "H14", "H12", "F17", "H16", "I9", "I8", "I14", "I11", "I10", "J6", "I15", "I13", "I12", "H17", "J15",
+    "J14", "J13", "J11", "J7", "J8", "J16", "J12", "J9", "J10", "J17",
 )
 
 

time: 81.2 us -> 83.3 us (1.026)
  Pallas kernels: 80.9 us -> 83 us
    pallas_call x1, Pallas kernels: 77.5 us -> 79.6 us  [step(): pl.pallas_call(functools.partial(kernel, n, mats, tokens, rows, cols), ou...]
where the time goes in v4:
time: 83.3 us; the launch traced here: 83.2 us
  Pallas kernels  83 us (100%)
    pallas_call x1, Pallas kernels, step(): pl.pallas_call(functools.partial(kernel, n, mats, tokens, rows, cols), ou...  79.6 us
    pallas_call x1, Pallas kernels, step(): pl.pallas_call(write, out_shape=jax.ShapeDtypeStruct((mats, rows, cols),...  3.4 us

profile of v4, /device:TPU:97, one launch (start us, length us, event | category | flops | bytes accessed | tf_op | source)
XLA Modules:
  0.0 83.2 jit_solution(10425151655334739814)
XLA Ops:
  0.0 79.6 %sums.1 = bf16[18,4,4,56,256]{4,3,2,1,0:T(8,128)(2,1)S(1)} custom-call(bf16[1,2,4096,896]{3,2,1,0:T(8,128)(2,1)} %a_ref.1, bf16[1,2,4096,2304]{3,2,1,0:T(8,128)(2,1)} %g_ref.1), custom_call_target="tpu_custom_call" | custom-call | tf_op jit(solution)/shard_map/sums/pallas_call | solution.py:355
  79.6 3.4 %write.1 = bf16[2,896,2304]{2,1,0:T(8,128)(2,1)} custom-call(bf16[18,896,256]{2,1,0:T(8,128)(2,1)S(1)} %bitcast.1), custom_call_target="tpu_custom_call" | custom-call | tf_op jit(solution)/shard_map/write/pallas_call | solution.py:388
